TPU v7x, 128 devices: a whole 4x4x4 slice. The times are simulated.
128 devices in a mesh: dp: 2 (over core), ep: 64 (over x, y, z).
Axes of the slice: x: 4, y: 4, z: 4, core: 2. Of those that a mesh axis runs over, the one named last changes fastest.
Arguments:
- x: bfloat16 [2, 64, 256, 1792], P('dp', 'ep'), parts along dimension 0
- expert: int32 [2, 64, 256, 8], P('dp', 'ep'), parts along dimension 0
- slot: int32 [2, 64, 256, 8], P('dp', 'ep'), parts along dimension 0
- gate: float32 [2, 64, 256, 8], P('dp', 'ep'), parts along dimension 0
- w_gate: bfloat16 [128, 1792, 2048], P('ep')
- w_up: bfloat16 [128, 1792, 2048], P('ep')
- w_down: bfloat16 [128, 2048, 1792], P('ep')
- s_gate: bfloat16 [1792, 2048], replicated
- s_up: bfloat16 [1792, 2048], replicated
- s_down: bfloat16 [2048, 1792], replicated
Outputs:
- y: bfloat16 [2, 64, 256, 1792], P('dp', 'ep'), parts along dimension 0
There are 2 independent parts. A program takes and returns all parts, laid end to end along the dimension named above; an argument that names none is the same for every part.
All inputs are finite; a program needn't handle non-finite values.
Results may differ from a plain program's by a relative error of at most 0.009.
Values are sent between devices in bfloat16 or wider.
A program may use at most 1.5 GiB of HBM per device.

v0:
```python
import jax
import jax.numpy as jnp
from jax import lax
from jax.sharding import NamedSharding, PartitionSpec as P


def einsum(form, a, b):
    return jnp.einsum(form, a.astype(jnp.float32), b.astype(jnp.float32))


def for_all(x, s_gate, s_up, s_down):
    h = jax.nn.silu(einsum("...d,df->...f", x, s_gate)) * einsum("...d,df->...f", x, s_up)
    return einsum("...f,fd->...d", h.astype(jnp.bfloat16), s_down)


def solution(mesh):
    def placed(v, *spec):
        return lax.with_sharding_constraint(v, NamedSharding(mesh, P(*spec)))

    def step(x, expert, slot, gate, w_gate, w_up, w_down, s_gate, s_up, s_down):
        experts, (tokens, top) = w_gate.shape[0], expert.shape[2:]
        slots = 5 * tokens * top // (4 * experts)
        to_expert = jax.nn.one_hot(expert, experts, dtype=jnp.bfloat16)
        to_slot = jax.nn.one_hot(slot, slots, dtype=jnp.bfloat16)
        weighted = to_expert * gate[..., None].astype(jnp.bfloat16)
        dispatch = einsum("abtke,abtkc->abtec", to_expert, to_slot).astype(jnp.bfloat16)
        combine = einsum("abtke,abtkc->abtec", weighted, to_slot).astype(jnp.bfloat16)
        z = einsum("abtec,abtd->aebcd", dispatch, x).astype(jnp.bfloat16)
        z = placed(z, "dp", None, "ep", None, None)
        z = placed(z, "dp", "ep", None, None, None)
        h = jax.nn.silu(einsum("aebcd,edf->aebcf", z, w_gate))
        h = (h * einsum("aebcd,edf->aebcf", z, w_up)).astype(jnp.bfloat16)
        out = einsum("aebcf,efd->aebcd", h, w_down).astype(jnp.bfloat16)
        out = placed(out, "dp", "ep", None, None, None)
        out = placed(out, "dp", None, "ep", None, None)
        y = einsum("abtec,aebcd->abtd", combine, out)
        return (y + for_all(x, s_gate, s_up, s_down)).astype(jnp.bfloat16)

    return step
```

profile of v0, /device:TPU:38, one launch (start us, length us, event | category | flops | bytes accessed | tf_op | source)
XLA Modules:
  0.0 473.9 jit_solution(17048740788517557655)
XLA Ops:
  0.0 0.0 copy-start
  0.0 0.9 copy.18
  0.9 0.8 copy.20
  1.8 0.0 copy-start.3
  1.8 2.8 convolution_convert_fusion.1
  4.6 0.0 copy-done
  4.6 6.2 %convolution_convert_fusion = bf16[128,20,1792]{2,0,1:T(8,128)(2,1)} fusion(bf16[256,128,20]{1,2,0:T(8,128)(2,1)S(1)} %convolution_convert_fusion.1, bf16[1,1,256,1792]{3,2,1,0:T(8,128)(2,1)S(1)} %copy-done), kind=kOutput, calls=%fused_computation.19 | convolution fusion | flops 2353397760 | bytes 11403264 | tf_op jit(solution)/abtec,abtd->aebcd/dot_general | solution.py:8
  10.8 18.6 %reshape.6 = bf16[1,64,2,1,20,1792]{5,2,1,4,3,0:T(2,128)(2,1)} reshape(bf16[128,20,1792]{2,0,1:T(8,128)(2,1)} %convolution_convert_fusion) | data formatting | bytes 18350080 | tf_op jit(solution)/sharding_constraint;jit(solution)/sharding_constraint | solution.py:18
  29.4 7.9 %copy.22 = bf16[1,64,2,1,20,1792]{5,2,4,3,0,1:T(2,128)(2,1)S(1)} copy(bf16[1,64,2,1,20,1792]{5,2,1,4,3,0:T(2,128)(2,1)} %reshape.6) | data formatting | bytes 18350080 | tf_op jit(solution)/sharding_constraint;jit(solution)/sharding_constraint | solution.py:18
  37.3 131.9 %all-to-all.4 = bf16[1,64,2,1,20,1792]{5,2,4,3,0,1:T(2,128)(2,1)} all-to-all(bf16[1,64,2,1,20,1792]{5,2,4,3,0,1:T(2,128)(2,1)S(1)} %copy.22), channel_id=1, replica_groups=mesh['dp'=2,'ep'=64] {'ep'}, dimensions={1} | all-to-all | bytes 18350080 | tf_op jit(solution)/sharding_constraint;jit(solution)/sharding_constraint | solution.py:18
  169.2 33.2 %fusion.6 = f32[2,64,20,2048]{3,1,2,0:T(8,128)} fusion(bf16[2,1792,2048]{2,1,0:T(8,128)(2,1)} %param.5, bf16[1,64,2,1,20,1792]{5,2,4,3,0,1:T(2,128)(2,1)} %all-to-all.4), kind=kOutput, calls=%fused_computation.9 | convolution fusion | flops 18790481920 | bytes 44826624 | tf_op jit(solution)/aebcd,edf->aebcf/dot_general | solution.py:8
  202.4 33.2 %fusion.8 = f32[2,64,20,2048]{3,1,2,0:T(8,128)} fusion(bf16[2,1792,2048]{2,1,0:T(8,128)(2,1)} %param.4, bf16[1,64,2,1,20,1792]{5,2,4,3,0,1:T(2,128)(2,1)} %all-to-all.4), kind=kOutput, calls=%fused_computation.11 | convolution fusion | flops 18790481920 | bytes 44826624 | tf_op jit(solution)/aebcd,edf->aebcf/dot_general | solution.py:8
  235.6 29.6 %convert_bitcast_fusion = bf16[1,2,64,1,20,1792]{5,2,4,1,3,0:T(8,128)(2,1)} fusion(bf16[2,2048,1792]{2,1,0:T(8,128)(2,1)} %param.6, f32[2,64,20,2048]{3,1,2,0:T(8,128)} %fusion.6, f32[2,64,20,2048]{3,1,2,0:T(8,128)} %fusion.8), kind=kOutput, calls=%fused_computation.16 | convolution fusion | flops 18826526720 | bytes 65798144 | tf_op jit(solution)/aebcf,efd->aebcd/dot_general | solution.py:8
  265.1 14.3 %copy.24 = bf16[1,2,64,1,20,1792]{5,1,4,3,0,2:T(2,128)(2,1)} copy(bf16[1,2,64,1,20,1792]{5,2,4,1,3,0:T(8,128)(2,1)} %convert_bitcast_fusion) | data formatting | bytes 18350080 | tf_op jit(solution)/sharding_constraint;jit(solution)/sharding_constraint | solution.py:18
  279.4 0.0 copy-start.4
  279.5 11.9 %all-to-all-start.1 = ((bf16[1,2,64,1,20,1792]{5,1,4,3,0,2:T(2,128)(2,1)}), bf16[1,2,64,1,20,1792]{5,1,4,3,0,2:T(2,128)(2,1)}, u32[]{:S(2)}, u32[]{:S(2)}) async-start(bf16[1,2,64,1,20,1792]{5,1,4,3,0,2:T(2,128)(2,1)} %copy.24), calls=%async_computation.1 | async-start | bytes 18350080 | tf_op jit(solution)/sharding_constraint;jit(solution)/sharding_constraint | solution.py:18
  291.3 0.1 copy.19
  291.5 3.2 convolution_convert_fusion.2
  294.7 6.5 %convolution_bitcast_fusion.1 = f32[1,1,256,2048]{3,2,1,0:T(8,128)} fusion(bf16[1792,2048]{1,0:T(8,128)(2,1)} %param.7, bf16[1,1,256,1792]{3,2,1,0:T(8,128)(2,1)S(1)} %copy-done), kind=kOutput, calls=%fused_computation.22 | convolution fusion | flops 1879048192 | bytes 10354688 | tf_op jit(solution)/...d,df->...f/dot_general | solution.py:8
  301.1 11.2 %fusion.38 = f32[256,1792]{1,0:T(8,128)} fusion(bf16[2048,1792]{1,0:T(8,128)(2,1)} %param.9, bf16[1792,2048]{1,0:T(8,128)(2,1)} %param.8, f32[1,1,256,2048]{3,2,1,0:T(8,128)} %convolution_bitcast_fusion.1, bf16[1,1,256,1792]{3,2,1,0:T(8,128)(2,1)S(1)} %copy-done), kind=kOutput, calls=%fused_computation.41 | convolution fusion | flops 3761242112 | bytes 19529728 | tf_op jit(solution)/...f,fd->...d/dot_general | solution.py:8
  312.3 126.8 %all-to-all-done.1 = bf16[1,2,64,1,20,1792]{5,1,4,3,0,2:T(2,128)(2,1)} async-done(((bf16[1,2,64,1,20,1792]{5,1,4,3,0,2:T(2,128)(2,1)}), bf16[1,2,64,1,20,1792]{5,1,4,3,0,2:T(2,128)(2,1)}, u32[]{:S(2)}, u32[]{:S(2)}) %all-to-all-start.1) | async-done | bytes 9175072 | tf_op jit(solution)/sharding_constraint;jit(solution)/sharding_constraint | solution.py:18
  439.1 8.7 %copy.25 = bf16[1,64,2,1,20,1792]{5,2,1,4,3,0:T(2,128)(2,1)} copy(bf16[1,64,2,1,20,1792]{5,2,4,3,0,1:T(2,128)(2,1)} %bitcast.21) | data formatting | bytes 18350080 | tf_op jit(solution)/sharding_constraint;jit(solution)/sharding_constraint | solution.py:18
  447.8 19.3 %reshape.46 = bf16[128,20,1792]{2,0,1:T(8,128)(2,1)} reshape(bf16[1,64,2,1,20,1792]{5,2,1,4,3,0:T(2,128)(2,1)} %copy.25) | data formatting | bytes 18350080
  467.2 6.8 %fusion.25 = bf16[1,1,256,1792]{3,2,1,0:T(8,128)(2,1)} fusion(f32[256,1792]{1,0:T(8,128)} %fusion.38, bf16[128,20,1792]{2,0,1:T(8,128)(2,1)} %reshape.46, bf16[256,128,20]{1,2,0:T(8,128)(2,1)S(1)} %convolution_convert_fusion.2), kind=kOutput, calls=%fused_computation.28 | convolution fusion | flops 2349727744 | bytes 13238272 | tf_op jit(solution)/abtec,aebcd->abtd/dot_general | solution.py:8
  (9 shorter events, 0.0 us)
Async XLA Ops:
  0.0 4.6 copy-start
  0.9 28.5 %copy-start.1 = (s32[256,8]{1,0:T(8,128)}, s32[256,8]{1,0:T(8,128)S(1)}, u32[]{:S(2)}) copy-start(s32[256,8]{1,0:T(8,128)S(1)} %copy.18) | copy-start | bytes 24580
  1.8 27.6 %copy-start.3 = (s32[256,8]{1,0:T(8,128)}, s32[256,8]{1,0:T(8,128)S(1)}, u32[]{:S(2)}) copy-start(s32[256,8]{1,0:T(8,128)S(1)} %copy.20) | copy-start | bytes 24580
  279.4 11.9 %copy-start.5 = (f32[1,1,256,8]{2,3,1,0:T(8,128)S(1)}, f32[1,1,256,8]{2,3,1,0:T(8,128)}, u32[]{:S(2)}) copy-start(f32[1,1,256,8]{2,3,1,0:T(8,128)} %param.1) | copy-start | bytes 24580
  279.4 12.0 %copy-start.2 = (s32[256,8]{1,0:T(8,128)S(1)}, s32[256,8]{1,0:T(8,128)}, u32[]{:S(2)}) copy-start(s32[256,8]{1,0:T(8,128)} %copy-done.1) | copy-start | bytes 24580
  279.4 12.0 %copy-start.4 = (s32[256,8]{1,0:T(8,128)S(1)}, s32[256,8]{1,0:T(8,128)}, u32[]{:S(2)}) copy-start(s32[256,8]{1,0:T(8,128)} %copy-done.3) | copy-start | bytes 24580
  279.5 159.6 %all-to-all-start.1 = ((bf16[1,2,64,1,20,1792]{5,1,4,3,0,2:T(2,128)(2,1)}), bf16[1,2,64,1,20,1792]{5,1,4,3,0,2:T(2,128)(2,1)}, u32[]{:S(2)}, u32[]{:S(2)}) async-start(bf16[1,2,64,1,20,1792]{5,1,4,3,0,2:T(2,128)(2,1)} %copy.24), calls=%async_computation.1 | async-start | bytes 18350080 | tf_op jit(solution)/sharding_constraint;jit(solution)/sharding_constraint | solution.py:18
where the time goes:
time: 475 us; the launch traced here: 474 us
  matrix products  133 us (28%)
  blocking collectives  132 us (28%)
  waiting for transfers between devices  127 us (27%)
  local copies, waits for them, and re-layouts  70.8 us (15%)
  starting transfers between devices  11.9 us (3%)
    dot_general x9, matrix products, einsum(): return jnp.einsum(form, a.astype(jnp.float32), b.astype(jnp.float32))  133 us
    another operation x1, blocking collectives, placed(): return lax.with_sharding_constraint(v, NamedSharding(mesh, P(*spec)))  132 us
    another operation x1, waiting for transfers between devices, placed(): return lax.with_sharding_constraint(v, NamedSharding(mesh, P(*spec)))  127 us
    another operation x4, local copies, waits for them, and re-layouts, placed(): return lax.with_sharding_constraint(v, NamedSharding(mesh, P(*spec)))  49.5 us
    unnamed x15, local copies, waits for them, and re-layouts  21.1 us
    another operation x1, starting transfers between devices, placed(): return lax.with_sharding_constraint(v, NamedSharding(mesh, P(*spec)))  11.9 us
  transfers between devices with their start and end apart: 1, of which 1 were waited for; matrix products, arithmetic and copies ran while one was open for 4% of the time, Pallas kernels for 0%

commit v1 on v0

v1 whole, which is shorter than its diff:
```python
import jax
import jax.numpy as jnp
from jax import lax
from jax.experimental import pallas as pl
from jax.experimental.pallas import tpu as pltpu
from jax.sharding import PartitionSpec as P

F32, BF16 = jnp.float32, jnp.bfloat16
T, D, FF, TOP, SLOTS = 256, 1792, 2048, 8, 20
GROUPS = 5
TILE = 256
STEPS = FF // TILE
BUFS = 3
LANES = ((0, 640), (640, 640), (1280, 512))
OTHERS = ((1, 2), (0, 2), (0, 1))
MESH = pl.DeviceIdType.MESH
OFFSETS = tuple((a, b) for a in range(4) for b in range(4) if (a, b) != (0, 0))


def part(p):
    return pl.ds(*LANES[p])


def contract_rows(a, b):
    return lax.dot_general(a, b, (((0,), (0,)), ((), ())), preferred_element_type=F32)


def dot(a, b):
    return jnp.dot(a, b, preferred_element_type=F32)


def kernel(x, expert, slot, gate, wg, wu, wd, sg, su, sd, y,
           lines, mine, tables, out_rows, z, back, acc, total, last, bg, bu, bd,
           s1, r1, st, rt, sz, rz, sc, rc, sl, rl, wsem):
    me = lax.axis_index("ep")
    coord = (me // 16, (me // 4) % 4, me % 4)

    def moved(p, by):
        c = list(coord)
        c[p] = (c[p] + by) % 4
        return c

    def device(c):
        return {"ep": c[0] * 16 + c[1] * 4 + c[2]}

    def send(src, dst, ss, rs, c):
        pltpu.make_async_remote_copy(src_ref=src, dst_ref=dst, send_sem=ss, recv_sem=rs,
                                     device_id=device(c), device_id_type=MESH).start()

    def wait(like, sem):
        pltpu.make_async_copy(like, like, sem).wait()

    def in_plane(p, c):
        return c[OTHERS[p][0]] * 4 + c[OTHERS[p][1]]

    def rows_of(p, g, c):
        at = [g, *c, slice(None), part(p)]
        at[1 + p] = slice(None)
        return tuple(at)

    def weights(n):
        b = n % BUFS

        @pl.when(n < STEPS)
        def _():
            f = pl.multiple_of(n * TILE, TILE)
            pltpu.make_async_copy(sg.at[:, pl.ds(f, TILE)], bg.at[b], wsem.at[b, 0]).start()
            pltpu.make_async_copy(su.at[:, pl.ds(f, TILE)], bu.at[b], wsem.at[b, 1]).start()
            pltpu.make_async_copy(sd.at[pl.ds(f, TILE), :], bd.at[b], wsem.at[b, 2]).start()

        @pl.when((n >= STEPS) & (n < 7 * STEPS))
        def _():
            e = (n - STEPS) // (3 * STEPS)
            f = pl.multiple_of((n % STEPS) * TILE, TILE)
            pltpu.make_async_copy(wg.at[e, :, pl.ds(f, TILE)], bg.at[b], wsem.at[b, 0]).start()
            pltpu.make_async_copy(wu.at[e, :, pl.ds(f, TILE)], bu.at[b], wsem.at[b, 1]).start()
            pltpu.make_async_copy(wd.at[e, pl.ds(f, TILE), :], bd.at[b], wsem.at[b, 2]).start()

    def ready(n):
        b = n % BUFS
        wait(bg.at[b], wsem.at[b, 0])
        wait(bu.at[b], wsem.at[b, 1])
        wait(bd.at[b], wsem.at[b, 2])
        return b

    weights(0)
    weights(1)
    for by in (2, 1, 3):
        for p in range(3):
            send(x.at[:, part(p)], lines.at[coord[p], :, part(p)], s1.at[p], r1.at[p], moved(p, by))
    for p in range(3):
        lines[coord[p], :, part(p)] = x[:, part(p)]

    ex, sl_ = expert[...], slot[...]
    dev, at = ex >> 1, (ex & 1) * SLOTS + sl_
    valid = sl_ < SLOTS
    c = (dev >> 4, (dev >> 2) & 3, dev & 3)
    g8, j8 = at >> 3, at & 7
    gates = gate[...].astype(BF16).astype(F32)
    number = lax.broadcasted_iota(jnp.int32, (T, 128), 0).astype(F32) + 1.0
    lane = lax.broadcasted_iota(jnp.int32, (T, 128), 1)
    for p in range(3):
        row = jnp.where(valid, c[p] * 8 + g8, -1)
        col = (c[OTHERS[p][0]] * 4 + c[OTHERS[p][1]]) * 8 + j8
        table = jnp.zeros((128, 256), F32)
        for k in range(TOP):
            left = (lane == row[:, k:k + 1]).astype(BF16)
            here = lane == col[:, k:k + 1]
            right = jnp.concatenate([jnp.where(here, number, 0.0), jnp.where(here, gates[:, k:k + 1], 0.0)], axis=1)
            table += contract_rows(left, right.astype(BF16))
        for i in range(4):
            mine[p, i, 0:8, :] = table[8 * i:8 * i + 8, :128]
            mine[p, i, 8:16, :] = table[8 * i:8 * i + 8, 128:]
        tables[p, coord[p]] = mine[p, coord[p]]
    for by in (2, 1, 3):
        for p in range(3):
            to = moved(p, by)
            send(mine.at[p, to[p]], tables.at[p, coord[p]], st.at[p], rt.at[p], to)

    total[...] = jnp.zeros_like(total)

    def shared(n, _):
        weights(n + 2)
        b = ready(n)
        h = jax.nn.silu(dot(x[...], bg[b])) * dot(x[...], bu[b])
        total[...] += dot(h.astype(BF16), bd[b])
        return 0

    lax.fori_loop(0, STEPS, shared, 0)
    for p in range(3):
        wait(lines.at[0:3, :, part(p)], r1.at[p])
        wait(tables.at[p, 0:3], rt.at[p])

    def dispatch(g):
        for p in range(3):
            for i in range(4):
                pick = (number == tables[p, i, pl.ds(g, 1), :]).astype(BF16)
                rows = contract_rows(pick, lines[i, :, part(p)]).astype(BF16)
                out_rows[g, i, :, :, part(p)] = rows.reshape(16, 8, LANES[p][1])
        for a, b in OFFSETS:
            for p in range(3):
                to = list(coord)
                to[OTHERS[p][0]] = (to[OTHERS[p][0]] + a) % 4
                to[OTHERS[p][1]] = (to[OTHERS[p][1]] + b) % 4
                send(out_rows.at[g, :, in_plane(p, to), :, part(p)], z.at[rows_of(p, g, coord)],
                     sz.at[g], rz.at[g], to)
        for p in range(3):
            z[rows_of(p, g, coord)] = out_rows[g, :, in_plane(p, coord), :, part(p)]

    def give_back(g):
        for a, b in OFFSETS:
            for p in range(3):
                to = list(coord)
                to[OTHERS[p][0]] = (to[OTHERS[p][0]] + a) % 4
                to[OTHERS[p][1]] = (to[OTHERS[p][1]] + b) % 4
                send(z.at[rows_of(p, g, to)], back.at[:, g, in_plane(p, coord), :, part(p)],
                     sc.at[g], rc.at[g], to)
        for p in range(3):
            back[:, g, in_plane(p, coord), :, part(p)] = z[rows_of(p, g, coord)]

    def experts(i):
        e = i // 3
        g = i - e

        @pl.when(i != 3)
        def _():
            wait(out_rows.at[g, :, 0:15], rz.at[g])
            acc[...] = jnp.zeros_like(acc)

        at = g * 8 + (lax.broadcasted_iota(jnp.int32, (512, TILE), 0) & 7)
        own = (at >= SLOTS) == (e == 1)

        def step(f, _):
            n = STEPS + i * STEPS + f
            weights(n + 2)
            b = ready(n)
            rows = z[g].reshape(512, D)
            h = jax.nn.silu(dot(rows, bg[b])) * dot(rows, bu[b])
            acc[...] += dot(jnp.where(own, h, 0.0).astype(BF16), bd[b])
            return 0

        lax.fori_loop(0, STEPS, step, 0)

        @pl.when(i != 2)
        def _():
            z[g] = acc[...].astype(BF16).reshape(4, 4, 4, 8, D)
            give_back(g)

    def turn(u, _):
        @pl.when(u < GROUPS)
        def _():
            dispatch(u)

        @pl.when(u >= 2)
        def _():
            experts(u - 2)

        return 0

    lax.fori_loop(0, 8, turn, 0)

    for g in range(GROUPS):
        wait(back.at[:, g, 0:15], rc.at[g])
    for by in (2, 1, 3, 0):
        for p in range(3):
            to = moved(p, by)
            i = to[p]
            mix = jnp.concatenate(
                [jnp.where(number == tables[p, i, g:g + 1, :], tables[p, i, 8 + g:9 + g, :], 0.0).astype(BF16)
                 for g in range(GROUPS)], axis=1)
            summed = dot(mix, back[i, :, :, :, part(p)].reshape(GROUPS * 128, LANES[p][1]))
            if by:
                lines[i, :, part(p)] = summed.astype(BF16)
                send(lines.at[i, :, part(p)], last.at[coord[p], :, part(p)], sl.at[p], rl.at[p], to)
            else:
                total[:, part(p)] += summed
    for p in range(3):
        wait(last.at[0:3, :, part(p)], rl.at[p])
        for by in (1, 2, 3):
            total[:, part(p)] += last[moved(p, by)[p], :, part(p)].astype(F32)
    y[...] = total[...].astype(BF16)

    for p in range(3):
        wait(lines.at[0:3, :, part(p)], s1.at[p])
        wait(tables.at[p, 0:3], st.at[p])
        wait(last.at[0:3, :, part(p)], sl.at[p])
    for g in range(GROUPS):
        wait(out_rows.at[g, :, 0:15], sz.at[g])
        wait(back.at[:, g, 0:15], sc.at[g])


def solution(mesh):
    dma = pltpu.SemaphoreType.DMA

    def body(x, expert, slot, gate, wg, wu, wd, sg, su, sd):
        vmem, anywhere = pl.BlockSpec(memory_space=pltpu.VMEM), pl.BlockSpec(memory_space=pl.ANY)
        out = pl.pallas_call(
            kernel,
            out_shape=jax.ShapeDtypeStruct((T, D), BF16),
            in_specs=[vmem] * 4 + [anywhere] * 6,
            out_specs=vmem,
            scratch_shapes=[
                pltpu.VMEM((4, T, D), BF16),
                pltpu.VMEM((3, 4, 16, 128), F32),
                pltpu.VMEM((3, 4, 16, 128), F32),
                pltpu.VMEM((GROUPS, 4, 16, 8, D), BF16),
                pltpu.VMEM((GROUPS, 4, 4, 4, 8, D), BF16),
                pltpu.VMEM((4, GROUPS, 16, 8, D), BF16),
                pltpu.VMEM((512, D), F32),
                pltpu.VMEM((T, D), F32),
                pltpu.VMEM((4, T, D), BF16),
                pltpu.VMEM((BUFS, D, TILE), BF16),
                pltpu.VMEM((BUFS, D, TILE), BF16),
                pltpu.VMEM((BUFS, TILE, D), BF16),
                dma((3,)), dma((3,)), dma((3,)), dma((3,)),
                dma((GROUPS,)), dma((GROUPS,)), dma((GROUPS,)), dma((GROUPS,)),
                dma((3,)), dma((3,)), dma((BUFS, 3)),
            ],
            compiler_params=pltpu.CompilerParams(has_side_effects=True, vmem_limit_bytes=67043328),
            name="moe",
        )(x[0, 0], expert[0, 0], slot[0, 0], gate[0, 0], wg, wu, wd, sg, su, sd)
        return out[None, None]

    tokens, experts = P("dp", "ep", None, None), P("ep", None, None)
    return jax.shard_map(body, mesh=mesh, in_specs=(tokens,) * 4 + (experts,) * 3 + (P(None, None),) * 3,
                         out_specs=tokens, check_vma=False)
```

time: 475 us -> 204 us (0.43)
  the two profiles are of different devices: /device:TPU:38 before, /device:TPU:1 now
where the time goes in v1:
time: 204 us
  Pallas kernels  197 us (97%)
  local copies, waits for them, and re-layouts  6.61 us (3%)
    pallas_call x1, Pallas kernels, body(): pl.pallas_call(kernel, out_shape=jax.ShapeDtypeStruct((T, D), BF16), in_s...  197 us
    unnamed x4, local copies, waits for them, and re-layouts  6.61 us

profile of v1, /device:TPU:1, one launch (start us, length us, event | category | flops | bytes accessed | tf_op | source)
XLA Modules:
  0.0 203.5 jit_solution(658220664614673884)
XLA Ops:
  0.0 1.5 copy.11
  1.5 1.5 copy.12
  3.0 1.5 copy.13
  4.5 196.9 %moe.1 = bf16[256,1792]{1,0:T(8,128)(2,1)} custom-call(bf16[256,1792]{1,0:T(8,128)(2,1)} %bitcast.6, s32[256,8]{1,0:T(8,128)} %bitcast.7, s32[256,8]{1,0:T(8,128)} %bitcast.8, f32[256,8]{1,0:T(8,128)} %bitcast.9, bf16[2,1792,2048]{2,1,0:T(8,128)(2,1)} %wg.1, bf16[2,1792,2048]{2,1,0:T(8,128)(2,1)} %wu.1, bf16[2,2048,1792]{2,1,0:T(8,128)(2,1)} %wd.1, ...), custom_call_target="tpu_custom_call" | custom-call | tf_op jit(solution)/shard_map/moe/pallas_call | solution.py:237
  201.3 2.2 %copy.15 = bf16[1,1,256,1792]{3,2,1,0:T(8,128)(2,1)} copy(bf16[1,1,256,1792]{3,2,1,0:T(8,128)(2,1)} %bitcast.5) | data formatting | bytes 1835008

commit v2 on v1

--- a/solution.py
+++ b/solution.py
@@ -13,7 +13,11 @@
 BUFS = 3
 LANES = ((0, 640), (640, 640), (1280, 512))
 OTHERS = ((1, 2), (0, 2), (0, 1))
+HALF = (slice(0, T // 2), slice(T // 2, T))
+TO_NEXT = ((1, 0), (3, 1), (1, 1), (3, 0))
+PASS_ON = 5
 MESH = pl.DeviceIdType.MESH
+NEAR = tuple((a, b, c) for a in range(4) for b in range(4) for c in range(4) if 0 in (a, b, c) and (a, b, c) != (0, 0, 0))
 OFFSETS = tuple((a, b) for a in range(4) for b in range(4) if (a, b) != (0, 0))
 
 
@@ -30,10 +34,15 @@
 
 
 def kernel(x, expert, slot, gate, wg, wu, wd, sg, su, sd, y,
-           lines, mine, tables, out_rows, z, back, acc, total, last, bg, bu, bd,
+           lines, mine, tables, out_rows, z, back, acc, total, hop, last, bg, bu, bd,
            s1, r1, st, rt, sz, rz, sc, rc, sl, rl, wsem):
-    me = lax.axis_index("ep")
-    coord = (me // 16, (me // 4) % 4, me % 4)
+    me, swap = lax.axis_index("ep"), lax.axis_index("dp") == 1
+
+    def coordinates(d):
+        u, v, w = d >> 4, (d >> 2) & 3, d & 3
+        return u, jnp.where(swap, w, v), jnp.where(swap, v, w)
+
+    coord = coordinates(me)
 
     def moved(p, by):
         c = list(coord)
@@ -41,7 +50,7 @@
         return c
 
     def device(c):
-        return {"ep": c[0] * 16 + c[1] * 4 + c[2]}
+        return {"ep": c[0] * 16 + jnp.where(swap, c[2] * 4 + c[1], c[1] * 4 + c[2])}
 
     def send(src, dst, ss, rs, c):
         pltpu.make_async_remote_copy(src_ref=src, dst_ref=dst, send_sem=ss, recv_sem=rs,
@@ -83,43 +92,63 @@
         wait(bd.at[b], wsem.at[b, 2])
         return b
 
+    entered = pltpu.get_barrier_semaphore()
+    for by in NEAR:
+        to = [(v + d) % 4 for v, d in zip(coord, by)]
+        pl.semaphore_signal(entered, inc=1, device_id=device(to), device_id_type=MESH)
     weights(0)
     weights(1)
-    for by in (2, 1, 3):
-        for p in range(3):
-            send(x.at[:, part(p)], lines.at[coord[p], :, part(p)], s1.at[p], r1.at[p], moved(p, by))
-    for p in range(3):
-        lines[coord[p], :, part(p)] = x[:, part(p)]
 
     ex, sl_ = expert[...], slot[...]
-    dev, at = ex >> 1, (ex & 1) * SLOTS + sl_
+    c, at = coordinates(ex >> 1), (ex & 1) * SLOTS + sl_
     valid = sl_ < SLOTS
-    c = (dev >> 4, (dev >> 2) & 3, dev & 3)
     g8, j8 = at >> 3, at & 7
     gates = gate[...].astype(BF16).astype(F32)
-    number = lax.broadcasted_iota(jnp.int32, (T, 128), 0).astype(F32) + 1.0
-    lane = lax.broadcasted_iota(jnp.int32, (T, 128), 1)
+    along = lax.broadcasted_iota(jnp.int32, (128, T), 1).astype(F32) + 1.0
+    down = lax.broadcasted_iota(jnp.int32, (128, T), 0)
     for p in range(3):
         row = jnp.where(valid, c[p] * 8 + g8, -1)
         col = (c[OTHERS[p][0]] * 4 + c[OTHERS[p][1]]) * 8 + j8
-        table = jnp.zeros((128, 256), F32)
+        table = jnp.zeros((32, 256), F32)
         for k in range(TOP):
-            left = (lane == row[:, k:k + 1]).astype(BF16)
-            here = lane == col[:, k:k + 1]
-            right = jnp.concatenate([jnp.where(here, number, 0.0), jnp.where(here, gates[:, k:k + 1], 0.0)], axis=1)
-            table += contract_rows(left, right.astype(BF16))
+            left = (down[:32] == row[k:k + 1, :]).astype(BF16)
+            here = down == col[k:k + 1, :]
+            right = jnp.concatenate([jnp.where(here, along, 0.0), jnp.where(here, gates[k:k + 1, :], 0.0)], axis=0)
+            table += lax.dot_general(left, right.astype(BF16), (((1,), (1,)), ((), ())), preferred_element_type=F32)
         for i in range(4):
             mine[p, i, 0:8, :] = table[8 * i:8 * i + 8, :128]
             mine[p, i, 8:16, :] = table[8 * i:8 * i + 8, 128:]
         tables[p, coord[p]] = mine[p, coord[p]]
+    number = lax.broadcasted_iota(jnp.int32, (T, 128), 0).astype(F32) + 1.0
+    pl.semaphore_wait(entered, len(NEAR))
+
     for by in (2, 1, 3):
         for p in range(3):
             to = moved(p, by)
             send(mine.at[p, to[p]], tables.at[p, coord[p]], st.at[p], rt.at[p], to)
+    for first, half in ((1, 0), (3, 1), (1, 1), (3, 0)):
+        for p in range(3):
+            k = TO_NEXT.index((first, half))
+            send(x.at[HALF[half], part(p)], lines.at[coord[p], HALF[half], part(p)],
+                 s1.at[p, k], r1.at[p, k], moved(p, first))
+    for p in range(3):
+        lines[coord[p], :, part(p)] = x[:, part(p)]
 
     total[...] = jnp.zeros_like(total)
 
+    def pass_on():
+        for k, (first, half) in enumerate(TO_NEXT[:2]):
+            for p in range(3):
+                i = moved(p, 4 - first)[p]
+                arrived = lines.at[i, HALF[half], part(p)]
+                wait(arrived, r1.at[p, k])
+                send(arrived, arrived, s1.at[p, 4 + k], r1.at[p, 4 + k], moved(p, first))
+
     def shared(n, _):
+        @pl.when(n == PASS_ON)
+        def _():
+            pass_on()
+
         weights(n + 2)
         b = ready(n)
         h = jax.nn.silu(dot(x[...], bg[b])) * dot(x[...], bu[b])
@@ -128,7 +157,8 @@
 
     lax.fori_loop(0, STEPS, shared, 0)
     for p in range(3):
-        wait(lines.at[0:3, :, part(p)], r1.at[p])
+        for k in range(2, 6):
+            wait(lines.at[0, HALF[0], part(p)], r1.at[p, k])
         wait(tables.at[p, 0:3], rt.at[p])
 
     def dispatch(g):
@@ -137,8 +167,7 @@
                 pick = (number == tables[p, i, pl.ds(g, 1), :]).astype(BF16)
                 rows = contract_rows(pick, lines[i, :, part(p)]).astype(BF16)
                 out_rows[g, i, :, :, part(p)] = rows.reshape(16, 8, LANES[p][1])
-        for a, b in OFFSETS:
-            for p in range(3):
+            for a, b in OFFSETS:
                 to = list(coord)
                 to[OTHERS[p][0]] = (to[OTHERS[p][0]] + a) % 4
                 to[OTHERS[p][1]] = (to[OTHERS[p][1]] + b) % 4
@@ -201,29 +230,52 @@
 
     for g in range(GROUPS):
         wait(back.at[:, g, 0:15], rc.at[g])
-    for by in (2, 1, 3, 0):
+    def summed(p, i):
+        mix = jnp.concatenate(
+            [jnp.where(number == tables[p, i, g:g + 1, :], tables[p, i, 8 + g:9 + g, :], 0.0).astype(BF16)
+             for g in range(GROUPS)], axis=1)
+        return dot(mix, back[i, :, :, :, part(p)].reshape(GROUPS * 128, LANES[p][1]))
+
+    for p in range(3):
+        for k in range(2):
+            wait(lines.at[0, HALF[0], part(p)], s1.at[p, 4 + k])
+    for p in range(3):
+        i = moved(p, 2)[p]
+        lines[i, :, part(p)] = summed(p, i).astype(BF16)
+        for k, by in enumerate((3, 1)):
+            send(lines.at[i, HALF[k], part(p)], hop.at[k, :, part(p)], sl.at[p, k], rl.at[p, k], moved(p, by))
+    for k, by in enumerate((3, 1)):
         for p in range(3):
             to = moved(p, by)
-            i = to[p]
-            mix = jnp.concatenate(
-                [jnp.where(number == tables[p, i, g:g + 1, :], tables[p, i, 8 + g:9 + g, :], 0.0).astype(BF16)
-                 for g in range(GROUPS)], axis=1)
-            summed = dot(mix, back[i, :, :, :, part(p)].reshape(GROUPS * 128, LANES[p][1]))
-            if by:
-                lines[i, :, part(p)] = summed.astype(BF16)
-                send(lines.at[i, :, part(p)], last.at[coord[p], :, part(p)], sl.at[p], rl.at[p], to)
-            else:
-                total[:, part(p)] += summed
-    for p in range(3):
-        wait(last.at[0:3, :, part(p)], rl.at[p])
-        for by in (1, 2, 3):
-            total[:, part(p)] += last[moved(p, by)[p], :, part(p)].astype(F32)
+            own = summed(p, to[p])
+            lines[to[p], HALF[1 - k], part(p)] = own[HALF[1 - k]].astype(BF16)
+            send(lines.at[to[p], HALF[1 - k], part(p)], last.at[k, HALF[1 - k], part(p)],
+                 sl.at[p, 2 + k], rl.at[p, 2 + k], to)
+            acc[HALF[k], part(p)] = own[HALF[k]]
+    for k, by in enumerate((3, 1)):
+        for p in range(3):
+            to = moved(p, by)
+            wait(hop.at[k, :, part(p)], rl.at[p, k])
+            both = acc[HALF[k], part(p)] + hop[k, :, part(p)].astype(F32)
+            lines[to[p], HALF[k], part(p)] = both.astype(BF16)
+            send(lines.at[to[p], HALF[k], part(p)], last.at[k, HALF[k], part(p)],
+                 sl.at[p, 4 + k], rl.at[p, 4 + k], to)
+    for p in range(3):
+        total[:, part(p)] += summed(p, coord[p])
+    for j in (2, 4):
+        for k in range(2):
+            half = HALF[1 - k] if j == 2 else HALF[k]
+            for p in range(3):
+                wait(last.at[k, half, part(p)], rl.at[p, j + k])
+                total[half, part(p)] += last[k, half, part(p)].astype(F32)
     y[...] = total[...].astype(BF16)
 
     for p in range(3):
-        wait(lines.at[0:3, :, part(p)], s1.at[p])
+        for k in range(6):
+            if k < 4:
+                wait(lines.at[0, HALF[0], part(p)], s1.at[p, k])
+            wait(lines.at[0, HALF[0], part(p)], sl.at[p, k])
         wait(tables.at[p, 0:3], st.at[p])
-        wait(last.at[0:3, :, part(p)], sl.at[p])
     for g in range(GROUPS):
         wait(out_rows.at[g, :, 0:15], sz.at[g])
         wait(back.at[:, g, 0:15], sc.at[g])
@@ -248,17 +300,18 @@
                 pltpu.VMEM((4, GROUPS, 16, 8, D), BF16),
                 pltpu.VMEM((512, D), F32),
                 pltpu.VMEM((T, D), F32),
-                pltpu.VMEM((4, T, D), BF16),
+                pltpu.VMEM((2, T // 2, D), BF16),
+                pltpu.VMEM((2, T, D), BF16),
                 pltpu.VMEM((BUFS, D, TILE), BF16),
                 pltpu.VMEM((BUFS, D, TILE), BF16),
                 pltpu.VMEM((BUFS, TILE, D), BF16),
-                dma((3,)), dma((3,)), dma((3,)), dma((3,)),
+                dma((3, 6)), dma((3, 6)), dma((3,)), dma((3,)),
                 dma((GROUPS,)), dma((GROUPS,)), dma((GROUPS,)), dma((GROUPS,)),
-                dma((3,)), dma((3,)), dma((BUFS, 3)),
+                dma((3, 6)), dma((3, 6)), dma((BUFS, 3)),
             ],
-            compiler_params=pltpu.CompilerParams(has_side_effects=True, vmem_limit_bytes=67043328),
+            compiler_params=pltpu.CompilerParams(has_side_effects=True, collective_id=0, vmem_limit_bytes=67043328),
             name="moe",
-        )(x[0, 0], expert[0, 0], slot[0, 0], gate[0, 0], wg, wu, wd, sg, su, sd)
+        )(x[0, 0], expert[0, 0].T, slot[0, 0].T, gate[0, 0].T, wg, wu, wd, sg, su, sd)
         return out[None, None]
 
     tokens, experts = P("dp", "ep", None, None), P("ep", None, None)

time: 204 us -> 189 us (0.926)
  Pallas kernels: 197 us -> 186 us
  local copies, waits for them, and re-layouts: 6.61 us -> 2.16 us
    pallas_call x1, Pallas kernels: 197 us -> 186 us  [body(): pl.pallas_call(kernel, out_shape=jax.ShapeDtypeStruct((T, D), BF16), in_s...]
    unnamed x4 -> x1, local copies, waits for them, and re-layouts: 6.61 us -> 2.16 us
where the time goes in v2:
time: 189 us
  Pallas kernels  186 us (98%)
  local copies, waits for them, and re-layouts  2.16 us (1%)
    pallas_call x1, Pallas kernels, body(): pl.pallas_call(kernel, out_shape=jax.ShapeDtypeStruct((T, D), BF16), in_s...  186 us

profile of v2, /device:TPU:1, one launch (start us, length us, event | category | flops | bytes accessed | tf_op | source)
XLA Modules:
  0.0 188.7 jit_solution(5563164074630706021)
XLA Ops:
  0.0 186.5 %moe.1 = bf16[256,1792]{1,0:T(8,128)(2,1)} custom-call(bf16[256,1792]{1,0:T(8,128)(2,1)} %bitcast.12, s32[8,256]{1,0:T(8,128)} %bitcast.13, s32[8,256]{1,0:T(8,128)} %bitcast.14, f32[8,256]{1,0:T(8,128)} %bitcast.15, bf16[2,1792,2048]{2,1,0:T(8,128)(2,1)} %wg.1, bf16[2,1792,2048]{2,1,0:T(8,128)(2,1)} %wu.1, bf16[2,2048,1792]{2,1,0:T(8,128)(2,1)} %wd.1, ...), custom_call_target="tpu_custom_call" | custom-call | tf_op jit(solution)/shard_map/moe/pallas_call | solution.py:289
  186.5 2.2 %copy.12 = bf16[1,1,256,1792]{3,2,1,0:T(8,128)(2,1)} copy(bf16[1,1,256,1792]{3,2,1,0:T(8,128)(2,1)} %bitcast.11) | data formatting | bytes 1835008

commit v3 on v2

--- a/solution.py
+++ b/solution.py
@@ -33,9 +33,9 @@
     return jnp.dot(a, b, preferred_element_type=F32)
 
 
-def kernel(x, expert, slot, gate, wg, wu, wd, sg, su, sd, y,
+def kernel(x_hbm, expert, slot, gate, wg, wu, wd, sg, su, sd, y,
            lines, mine, tables, out_rows, z, back, acc, total, hop, last, bg, bu, bd,
-           s1, r1, st, rt, sz, rz, sc, rc, sl, rl, wsem):
+           s1, r1, st, rt, sz, rz, sc, rc, sl, rl, wsem, x, xsem):
     me, swap = lax.axis_index("ep"), lax.axis_index("dp") == 1
 
     def coordinates(d):
@@ -91,6 +91,8 @@
         wait(bu.at[b], wsem.at[b, 1])
         wait(bd.at[b], wsem.at[b, 2])
         return b
+
+    pltpu.make_async_copy(x_hbm, x, xsem).start()
 
     entered = pltpu.get_barrier_semaphore()
     for by in NEAR:
@@ -120,6 +122,7 @@
             mine[p, i, 8:16, :] = table[8 * i:8 * i + 8, 128:]
         tables[p, coord[p]] = mine[p, coord[p]]
     number = lax.broadcasted_iota(jnp.int32, (T, 128), 0).astype(F32) + 1.0
+    wait(x, xsem)
     pl.semaphore_wait(entered, len(NEAR))
 
     for by in (2, 1, 3):
@@ -156,25 +159,43 @@
         return 0
 
     lax.fori_loop(0, STEPS, shared, 0)
-    for p in range(3):
-        for k in range(2, 6):
-            wait(lines.at[0, HALF[0], part(p)], r1.at[p, k])
-        wait(tables.at[p, 0:3], rt.at[p])
+    def plane(p):
+        for a, b in OFFSETS:
+            to = list(coord)
+            to[OTHERS[p][0]] = (to[OTHERS[p][0]] + a) % 4
+            to[OTHERS[p][1]] = (to[OTHERS[p][1]] + b) % 4
+            yield to
+
+    def pick(p, g, i):
+        chosen = (number == tables[p, i, pl.ds(g, 1), :]).astype(BF16)
+        rows = contract_rows(chosen, lines[i, :, part(p)]).astype(BF16)
+        out_rows[g, i, :, :, part(p)] = rows.reshape(16, 8, LANES[p][1])
+
+    def keep(g):
+        for p in range(3):
+            z[rows_of(p, g, coord)] = out_rows[g, :, in_plane(p, coord), :, part(p)]
 
     def dispatch(g):
         for p in range(3):
             for i in range(4):
-                pick = (number == tables[p, i, pl.ds(g, 1), :]).astype(BF16)
-                rows = contract_rows(pick, lines[i, :, part(p)]).astype(BF16)
-                out_rows[g, i, :, :, part(p)] = rows.reshape(16, 8, LANES[p][1])
-            for a, b in OFFSETS:
-                to = list(coord)
-                to[OTHERS[p][0]] = (to[OTHERS[p][0]] + a) % 4
-                to[OTHERS[p][1]] = (to[OTHERS[p][1]] + b) % 4
+                pick(p, g, i)
+            for to in plane(p):
                 send(out_rows.at[g, :, in_plane(p, to), :, part(p)], z.at[rows_of(p, g, coord)],
                      sz.at[g], rz.at[g], to)
-        for p in range(3):
-            z[rows_of(p, g, coord)] = out_rows[g, :, in_plane(p, coord), :, part(p)]
+        keep(g)
+
+    for by, arrivals in ((0, ()), (1, (3,)), (3, (2,)), (2, (4, 5))):
+        for p in range(3):
+            source = moved(p, by)
+            if by == 1:
+                wait(tables.at[p, 0:3], rt.at[p])
+            for k in arrivals:
+                wait(lines.at[0, HALF[0], part(p)], r1.at[p, k])
+            pick(p, 0, source[p])
+            for to in plane(p):
+                send(out_rows.at[0, source[p], in_plane(p, to), :, part(p)], z.at[(0, *source, slice(None), part(p))],
+                     sz.at[0], rz.at[0], to)
+    keep(0)
 
     def give_back(g):
         for a, b in OFFSETS:
@@ -215,18 +236,15 @@
             z[g] = acc[...].astype(BF16).reshape(4, 4, 4, 8, D)
             give_back(g)
 
-    def turn(u, _):
-        @pl.when(u < GROUPS)
-        def _():
-            dispatch(u)
-
-        @pl.when(u >= 2)
-        def _():
-            experts(u - 2)
-
-        return 0
-
-    lax.fori_loop(0, 8, turn, 0)
+    def each(f):
+        def run(i, _):
+            f(i)
+            return 0
+
+        return run
+
+    lax.fori_loop(1, GROUPS, each(dispatch), 0)
+    lax.fori_loop(0, GROUPS + 1, each(experts), 0)
 
     for g in range(GROUPS):
         wait(back.at[:, g, 0:15], rc.at[g])
@@ -289,7 +307,7 @@
         out = pl.pallas_call(
             kernel,
             out_shape=jax.ShapeDtypeStruct((T, D), BF16),
-            in_specs=[vmem] * 4 + [anywhere] * 6,
+            in_specs=[anywhere] + [vmem] * 3 + [anywhere] * 6,
             out_specs=vmem,
             scratch_shapes=[
                 pltpu.VMEM((4, T, D), BF16),
@@ -308,6 +326,7 @@
                 dma((3, 6)), dma((3, 6)), dma((3,)), dma((3,)),
                 dma((GROUPS,)), dma((GROUPS,)), dma((GROUPS,)), dma((GROUPS,)),
                 dma((3, 6)), dma((3, 6)), dma((BUFS, 3)),
+                pltpu.VMEM((T, D), BF16), dma(()),
             ],
             compiler_params=pltpu.CompilerParams(has_side_effects=True, collective_id=0, vmem_limit_bytes=67043328),
             name="moe",

time: 189 us -> 182 us (0.963)
  Pallas kernels: 186 us -> 179 us
    pallas_call x1, Pallas kernels: 186 us -> 179 us  [body(): pl.pallas_call(kernel, out_shape=jax.ShapeDtypeStruct((T, D), BF16), in_s...]
where the time goes in v3:
time: 182 us; the launch traced here: 181 us
  Pallas kernels  179 us (98%)
  local copies, waits for them, and re-layouts  2.16 us (1%)
    pallas_call x1, Pallas kernels, body(): pl.pallas_call(kernel, out_shape=jax.ShapeDtypeStruct((T, D), BF16), in_s...  179 us

profile of v3, /device:TPU:1, one launch (start us, length us, event | category | flops | bytes accessed | tf_op | source)
XLA Modules:
  0.0 181.4 jit_solution(14257867075140422545)
XLA Ops:
  0.0 179.2 %moe.1 = bf16[256,1792]{1,0:T(8,128)(2,1)} custom-call(bf16[256,1792]{1,0:T(8,128)(2,1)} %bitcast.12, s32[8,256]{1,0:T(8,128)} %bitcast.13, s32[8,256]{1,0:T(8,128)} %bitcast.14, f32[8,256]{1,0:T(8,128)} %bitcast.15, bf16[2,1792,2048]{2,1,0:T(8,128)(2,1)} %wg.1, bf16[2,1792,2048]{2,1,0:T(8,128)(2,1)} %wu.1, bf16[2,2048,1792]{2,1,0:T(8,128)(2,1)} %wd.1, ...), custom_call_target="tpu_custom_call" | custom-call | tf_op jit(solution)/shard_map/moe/pallas_call | solution.py:307
  179.2 2.2 %copy.12 = bf16[1,1,256,1792]{3,2,1,0:T(8,128)(2,1)} copy(bf16[1,1,256,1792]{3,2,1,0:T(8,128)(2,1)} %bitcast.11) | data formatting | bytes 1835008

commit v4 on v3

--- a/solution.py
+++ b/solution.py
@@ -33,9 +33,9 @@
     return jnp.dot(a, b, preferred_element_type=F32)
 
 
-def kernel(x_hbm, expert, slot, gate, wg, wu, wd, sg, su, sd, y,
+def kernel(x_hbm, e_hbm, s_hbm, g_hbm, wg, wu, wd, sg, su, sd, y_hbm,
            lines, mine, tables, out_rows, z, back, acc, total, hop, last, bg, bu, bd,
-           s1, r1, st, rt, sz, rz, sc, rc, sl, rl, wsem, x, xsem):
+           s1, r1, st, rt, sz, rz, sc, rc, sl, rl, wsem, x, xsem, expert, slot, gate, esem, y, ysem):
     me, swap = lax.axis_index("ep"), lax.axis_index("dp") == 1
 
     def coordinates(d):
@@ -92,15 +92,20 @@
         wait(bd.at[b], wsem.at[b, 2])
         return b
 
-    pltpu.make_async_copy(x_hbm, x, xsem).start()
-
     entered = pltpu.get_barrier_semaphore()
     for by in NEAR:
         to = [(v + d) % 4 for v, d in zip(coord, by)]
         pl.semaphore_signal(entered, inc=1, device_id=device(to), device_id_type=MESH)
+    routing = tuple(pltpu.make_async_copy(a, b, esem.at[n])
+                    for n, (a, b) in enumerate(((e_hbm, expert), (s_hbm, slot), (g_hbm, gate))))
+    for copy in routing:
+        copy.start()
+    pltpu.make_async_copy(x_hbm, x, xsem).start()
     weights(0)
     weights(1)
 
+    for copy in routing:
+        copy.wait()
     ex, sl_ = expert[...], slot[...]
     c, at = coordinates(ex >> 1), (ex & 1) * SLOTS + sl_
     valid = sl_ < SLOTS
@@ -285,8 +290,15 @@
             half = HALF[1 - k] if j == 2 else HALF[k]
             for p in range(3):
                 wait(last.at[k, half, part(p)], rl.at[p, j + k])
-                total[half, part(p)] += last[k, half, part(p)].astype(F32)
-    y[...] = total[...].astype(BF16)
+                both = total[half, part(p)] + last[k, half, part(p)].astype(F32)
+                if j == 2:
+                    total[half, part(p)] = both
+                else:
+                    y[half, part(p)] = both.astype(BF16)
+                    pltpu.make_async_copy(y.at[half, part(p)], y_hbm.at[half, part(p)], ysem.at[k, p]).start()
+    for k in range(2):
+        for p in range(3):
+            wait(y.at[HALF[k], part(p)], ysem.at[k, p])
 
     for p in range(3):
         for k in range(6):
@@ -303,12 +315,12 @@
     dma = pltpu.SemaphoreType.DMA
 
     def body(x, expert, slot, gate, wg, wu, wd, sg, su, sd):
-        vmem, anywhere = pl.BlockSpec(memory_space=pltpu.VMEM), pl.BlockSpec(memory_space=pl.ANY)
+        anywhere = pl.BlockSpec(memory_space=pl.ANY)
         out = pl.pallas_call(
             kernel,
             out_shape=jax.ShapeDtypeStruct((T, D), BF16),
-            in_specs=[anywhere] + [vmem] * 3 + [anywhere] * 6,
-            out_specs=vmem,
+            in_specs=[anywhere] * 10,
+            out_specs=anywhere,
             scratch_shapes=[
                 pltpu.VMEM((4, T, D), BF16),
                 pltpu.VMEM((3, 4, 16, 128), F32),
@@ -327,6 +339,8 @@
                 dma((GROUPS,)), dma((GROUPS,)), dma((GROUPS,)), dma((GROUPS,)),
                 dma((3, 6)), dma((3, 6)), dma((BUFS, 3)),
                 pltpu.VMEM((T, D), BF16), dma(()),
+                pltpu.VMEM((TOP, T), jnp.int32), pltpu.VMEM((TOP, T), jnp.int32), pltpu.VMEM((TOP, T), F32), dma((3,)),
+                pltpu.VMEM((T, D), BF16), dma((2, 3)),
             ],
             compiler_params=pltpu.CompilerParams(has_side_effects=True, collective_id=0, vmem_limit_bytes=67043328),
             name="moe",

time: 182 us -> 182 us (level)
  no operation moved by 1% of the time
where the time goes in v4:
time: 182 us; the launch traced here: 181 us
  Pallas kernels  179 us (98%)
  local copies, waits for them, and re-layouts  2.16 us (1%)
    pallas_call x1, Pallas kernels, body(): pl.pallas_call(kernel, out_shape=jax.ShapeDtypeStruct((T, D), BF16), in_s...  179 us

profile of v4, /device:TPU:1, one launch (start us, length us, event | category | flops | bytes accessed | tf_op | source)
XLA Modules:
  0.0 181.4 jit_solution(14305487354122911735)
XLA Ops:
  0.0 179.2 %moe.1 = bf16[256,1792]{1,0:T(8,128)(2,1)} custom-call(bf16[256,1792]{1,0:T(8,128)(2,1)} %bitcast.12, s32[8,256]{1,0:T(8,128)} %bitcast.13, s32[8,256]{1,0:T(8,128)} %bitcast.14, f32[8,256]{1,0:T(8,128)} %bitcast.15, bf16[2,1792,2048]{2,1,0:T(8,128)(2,1)} %wg.1, bf16[2,1792,2048]{2,1,0:T(8,128)(2,1)} %wu.1, bf16[2,2048,1792]{2,1,0:T(8,128)(2,1)} %wd.1, ...), custom_call_target="tpu_custom_call" | custom-call | tf_op jit(solution)/shard_map/moe/pallas_call | solution.py:319
  179.2 2.2 %copy.12 = bf16[1,1,256,1792]{3,2,1,0:T(8,128)(2,1)} copy(bf16[1,1,256,1792]{3,2,1,0:T(8,128)(2,1)} %bitcast.11) | data formatting | bytes 1835008

commit v5 on v4

--- a/solution.py
+++ b/solution.py
@@ -17,7 +17,6 @@
 TO_NEXT = ((1, 0), (3, 1), (1, 1), (3, 0))
 PASS_ON = 5
 MESH = pl.DeviceIdType.MESH
-NEAR = tuple((a, b, c) for a in range(4) for b in range(4) for c in range(4) if 0 in (a, b, c) and (a, b, c) != (0, 0, 0))
 OFFSETS = tuple((a, b) for a in range(4) for b in range(4) if (a, b) != (0, 0))
 
 
@@ -35,7 +34,7 @@
 
 def kernel(x_hbm, e_hbm, s_hbm, g_hbm, wg, wu, wd, sg, su, sd, y_hbm,
            lines, mine, tables, out_rows, z, back, acc, total, hop, last, bg, bu, bd,
-           s1, r1, st, rt, sz, rz, sc, rc, sl, rl, wsem, x, xsem, expert, slot, gate, esem, y, ysem):
+           s1, r1, st, rt, sz, rz, sc, rc, sl, rl, wsem, x, xsem, expert, slot, gate, esem, y, ysem, met):
     me, swap = lax.axis_index("ep"), lax.axis_index("dp") == 1
 
     def coordinates(d):
@@ -93,8 +92,8 @@
         return b
 
     entered = pltpu.get_barrier_semaphore()
-    for by in NEAR:
-        to = [(v + d) % 4 for v, d in zip(coord, by)]
+    peers = [moved(p, by) for p in range(3) for by in (1, 2, 3)]
+    for to in peers:
         pl.semaphore_signal(entered, inc=1, device_id=device(to), device_id_type=MESH)
     routing = tuple(pltpu.make_async_copy(a, b, esem.at[n])
                     for n, (a, b) in enumerate(((e_hbm, expert), (s_hbm, slot), (g_hbm, gate))))
@@ -128,7 +127,9 @@
         tables[p, coord[p]] = mine[p, coord[p]]
     number = lax.broadcasted_iota(jnp.int32, (T, 128), 0).astype(F32) + 1.0
     wait(x, xsem)
-    pl.semaphore_wait(entered, len(NEAR))
+    pl.semaphore_wait(entered, len(peers))
+    for to in peers:
+        pl.semaphore_signal(met, inc=1, device_id=device(to), device_id_type=MESH)
 
     for by in (2, 1, 3):
         for p in range(3):
@@ -188,6 +189,8 @@
                 send(out_rows.at[g, :, in_plane(p, to), :, part(p)], z.at[rows_of(p, g, coord)],
                      sz.at[g], rz.at[g], to)
         keep(g)
+
+    pl.semaphore_wait(met, len(peers))
 
     for by, arrivals in ((0, ()), (1, (3,)), (3, (2,)), (2, (4, 5))):
         for p in range(3):
@@ -340,7 +343,7 @@
                 dma((3, 6)), dma((3, 6)), dma((BUFS, 3)),
                 pltpu.VMEM((T, D), BF16), dma(()),
                 pltpu.VMEM((TOP, T), jnp.int32), pltpu.VMEM((TOP, T), jnp.int32), pltpu.VMEM((TOP, T), F32), dma((3,)),
-                pltpu.VMEM((T, D), BF16), dma((2, 3)),
+                pltpu.VMEM((T, D), BF16), dma((2, 3)), pltpu.SemaphoreType.REGULAR,
             ],
             compiler_params=pltpu.CompilerParams(has_side_effects=True, collective_id=0, vmem_limit_bytes=67043328),
             name="moe",

time: 182 us -> 186 us (1.022)
  the two profiles are of different devices: /device:TPU:1 before, /device:TPU:0 now
where the time goes in v5:
time: 186 us
  Pallas kernels  184 us (99%)
  local copies, waits for them, and re-layouts  2.16 us (1%)
    pallas_call x1, Pallas kernels, body(): pl.pallas_call(kernel, out_shape=jax.ShapeDtypeStruct((T, D), BF16), in_s...  184 us

profile of v5, /device:TPU:0, one launch (start us, length us, event | category | flops | bytes accessed | tf_op | source)
XLA Modules:
  0.0 186.0 jit_solution(5683353637345989421)
XLA Ops:
  0.0 183.8 %moe.1 = bf16[256,1792]{1,0:T(8,128)(2,1)} custom-call(bf16[256,1792]{1,0:T(8,128)(2,1)} %bitcast.12, s32[8,256]{1,0:T(8,128)} %bitcast.13, s32[8,256]{1,0:T(8,128)} %bitcast.14, f32[8,256]{1,0:T(8,128)} %bitcast.15, bf16[2,1792,2048]{2,1,0:T(8,128)(2,1)} %wg.1, bf16[2,1792,2048]{2,1,0:T(8,128)(2,1)} %wu.1, bf16[2,2048,1792]{2,1,0:T(8,128)(2,1)} %wd.1, ...), custom_call_target="tpu_custom_call" | custom-call | tf_op jit(solution)/shard_map/moe/pallas_call | solution.py:322
  183.8 2.2 %copy.12 = bf16[1,1,256,1792]{3,2,1,0:T(8,128)(2,1)} copy(bf16[1,1,256,1792]{3,2,1,0:T(8,128)(2,1)} %bitcast.11) | data formatting | bytes 1835008
